TPU v7x, 256 devices: a whole 4x4x8 slice. The times are simulated.
256 devices in a mesh: dp: 8 (over z), expert: 32 (over x, y, core).
Axes of the slice: x: 4, y: 4, z: 8, core: 2. Of those that a mesh axis runs over, the one named last changes fastest.
Arguments:
- tokens: bfloat16 [65536, 2048], P(('dp', 'expert')), may hold values from -6 to 6
- expert_ranks: int32 [32, 65536], P(None, ('dp', 'expert')), may hold values from 0 to 65535, as said below
- capacity: int32 [32], replicated, may hold values from 512 to 1024, as said below
- weight_in: bfloat16 [32, 2048, 8192], P('expert', None, 'dp'), may hold values from -0.125 to 0.125
- weight_out: bfloat16 [32, 8192, 2048], P('expert', 'dp'), may hold values from -0.0625 to 0.0625
- gate_weights: float32 [32, 1024], P('expert', 'dp'), may hold values from 0.05 to 1
Outputs:
- combined: bfloat16 [65536, 2048], P(('dp', 'expert'))
Inputs may be any that keep to these rules, and one draw needn't show every extreme that they name: `expert_ranks`: for each expert the ranks are a permutation of 0 to 65535. Of the 256 tokens of one device, at most 8 have rank under 1024 for one expert; for an expert of capacity 1024, some devices have exactly 8. At least one expert has capacity 1024.
All inputs are finite; a program needn't handle non-finite values.
Results may differ from a plain program's by a relative error of at most 0.0053.
Values may be sent and summed in bfloat16 or wider, within the bound.
No kernel may reach another device: no remote copies, remote signals or barrier semaphores. Data moves between devices by JAX's collectives and lax.ppermute only.
A program may use at most 64 MiB of HBM per device.

v0:
```python
import jax
import jax.numpy as jnp
from jax import lax
from jax.sharding import Mesh
from jax.sharding import PartitionSpec as P

MOST = 8
EXPERT = ("expert_0", "expert_1", "expert_2")
DP_EXPERT = ("dp", "expert_0", "expert_1", "expert_2")


def exclusive(values):
    return jnp.cumsum(values) - values


def on_device(tokens, expert_ranks, capacity, weight_in, weight_out, gate_weights):
    dp_count = lax.axis_size("dp")
    expert_count = lax.axis_size(EXPERT)
    token_count, width = tokens.shape
    slots_dp = gate_weights.shape[1]
    rows_all = expert_count * MOST
    own_dp = lax.axis_index("dp")
    own_expert = lax.axis_index(EXPERT)
    chosen = expert_ranks < capacity[:, None]
    chosen_int = chosen.astype(jnp.int32)
    counts = jnp.sum(chosen_int, axis=1)
    before = jnp.cumsum(chosen_int, axis=1) - chosen_int
    places = lax.broadcasted_iota(jnp.int32, (expert_count, MOST, token_count), 1)
    pack_table = jnp.logical_and(chosen[:, None, :], before[:, None, :] == places)
    pack_table = pack_table.astype(jnp.bfloat16).reshape(rows_all, token_count)
    packed = jnp.dot(pack_table, tokens, preferred_element_type=jnp.float32).astype(jnp.bfloat16)
    arrived_rows = lax.all_to_all(
        packed.reshape(expert_count, MOST, width), EXPERT, split_axis=0, concat_axis=0, tiled=True
    ).reshape(rows_all, width)
    device_ids = lax.broadcasted_iota(jnp.int32, (expert_count, expert_count), 0)
    expert_ids = lax.broadcasted_iota(jnp.int32, (expert_count, expert_count), 1)
    table = lax.psum(jnp.where(device_ids == own_expert, counts[None, :], 0), EXPERT)
    plane_ids = lax.broadcasted_iota(jnp.int32, (dp_count, expert_count), 0)
    plane_counts = lax.psum(
        jnp.where(plane_ids == own_dp, jnp.sum(table, axis=0)[None, :], 0), "dp"
    )
    most_rows = jnp.max(plane_counts)
    arrived = jnp.sum(jnp.where(expert_ids == own_expert, table, 0), axis=1)
    earlier = jnp.logical_and(plane_ids < own_dp, expert_ids[:dp_count] == own_expert)
    first_slot = jnp.sum(jnp.where(earlier, plane_counts, 0))
    within = lax.broadcasted_iota(jnp.int32, (expert_count, MOST), 1)
    target = jnp.where(within < arrived[:, None], exclusive(arrived)[:, None] + within, -1).reshape(
        rows_all
    )
    gates_all = lax.all_gather(gate_weights[0], "dp", axis=0, tiled=True)
    gates_all = jnp.concatenate([gates_all, jnp.zeros((rows_all,), gates_all.dtype)])

    def experts(rows, plane_rows):
        slot_ids = lax.broadcasted_iota(jnp.int32, (rows_all, plane_rows), 1)
        place_table = (target[:, None] == slot_ids).astype(jnp.bfloat16)
        plane = lax.dot_general(
            place_table, rows, (((0,), (0,)), ((), ())), preferred_element_type=jnp.float32
        ).astype(jnp.bfloat16)
        slot_rows = lax.all_gather(plane, "dp", axis=0, tiled=True)
        hidden = jnp.maximum(
            jnp.dot(slot_rows, weight_in[0], preferred_element_type=jnp.float32), 0.0
        ).astype(jnp.bfloat16)
        share = jnp.dot(hidden, weight_out[0], preferred_element_type=jnp.float32)
        out = lax.psum_scatter(
            share.astype(jnp.bfloat16), "dp", scatter_dimension=0, tiled=True
        ).astype(jnp.float32)
        gates = lax.dynamic_slice_in_dim(gates_all, first_slot, plane_rows, 0)
        scaled = (gates[:, None] * out).astype(jnp.bfloat16)
        returned = jnp.dot(place_table, scaled, preferred_element_type=jnp.float32)
        return returned.astype(jnp.bfloat16)

    fair = slots_dp + slots_dp // 4
    sent_back = lax.cond(
        most_rows <= fair,
        lambda rows: experts(rows, fair),
        lambda rows: experts(rows, rows_all),
        arrived_rows,
    )
    results = lax.all_to_all(
        sent_back.reshape(expert_count, MOST, width),
        EXPERT,
        split_axis=0,
        concat_axis=0,
        tiled=True,
    ).reshape(rows_all, width)
    combined = lax.dot_general(
        pack_table, results, (((0,), (0,)), ((), ())), preferred_element_type=jnp.float32
    )
    return combined.astype(jnp.bfloat16)


def solution(mesh):
    split = Mesh(
        mesh.devices.reshape(mesh.shape["dp"], 4, 4, 2), ("dp", "expert_0", "expert_1", "expert_2")
    )
    placed = (
        P(DP_EXPERT, None),
        P(None, DP_EXPERT),
        P(),
        P(EXPERT, None, "dp"),
        P(EXPERT, "dp", None),
        P(EXPERT, "dp"),
    )
    return jax.shard_map(
        on_device, mesh=split, in_specs=placed, out_specs=P(DP_EXPERT, None), check_vma=False
    )
```

profile of v0, /device:TPU:1, one launch (start us, length us, event | category | flops | bytes accessed | tf_op | source)
XLA Modules:
  0.0 359.8 jit_solution(15286796204240877624)
XLA Ops:
  6.5 0.0 copy-start
  6.5 0.0 copy-start.1
  6.5 0.9 convert_bitcast_fusion.1
  7.5 0.6 reduce-window.11
  8.1 0.2 slice_reduce_fusion
  8.3 0.1 iota.68
  8.4 0.1 convert_subtract_fusion
  8.5 0.0 copy-done
  8.5 1.5 fusion.21
  10.0 8.6 %all-to-all-start = ((bf16[32,8,2048]{2,1,0:T(8,128)(2,1)}), bf16[32,8,2048]{2,1,0:T(8,128)(2,1)S(1)}, u32[]{:S(2)}, u32[]{:S(2)}) async-start(bf16[32,8,2048]{2,1,0:T(8,128)(2,1)} %fusion.21), calls=%async_computation.2 | async-start | bytes 2097152 | tf_op jit(solution)/shard_map/all_to_all | solution.py:32
  18.6 0.1 broadcast_select_fusion
  18.7 127.2 %psum.14 = s32[32,32]{1,0:T(8,128)S(1)} all-reduce(s32[32,32]{1,0:T(8,128)S(1)} %broadcast_select_fusion), channel_id=1, replica_groups=mesh['dp'=8,'expert_0'=4,'expert_1'=4,'expert_2'=2] {'expert_0','expert_..., use_global_device_ids=true, to_apply=%region_3.4 | all-reduce | flops 1024 | bytes 8192 | tf_op jit(solution)/shard_map/psum | solution.py:37
  145.9 0.1 select_reduce_fusion.2
  146.0 0.1 broadcast_select_fusion.1
  146.1 13.5 %psum.15 = s32[8,32]{1,0:T(8,128)S(1)} all-reduce(s32[8,32]{1,0:T(8,128)S(1)} %broadcast_select_fusion.1), channel_id=1, replica_groups=mesh['dp'=8,'expert_0'=4,'expert_1'=4,'expert_2'=2] {'dp'}, use_global_device_ids=true, to_apply=%region_5.6 | all-reduce | flops 256 | bytes 2048 | tf_op jit(solution)/shard_map/psum | solution.py:39
  159.6 0.7 reduce_max.9
  161.0 0.1 copy.25
  161.1 0.1 reduce-window.18
  161.2 0.0 copy-done.1
  161.2 10.9 %all-gather = f32[1,1024]{1,0:T(1,128)S(1)} all-gather(f32[1,128]{1,0:T(1,128)S(1)} %copy-done.1), channel_id=2, replica_groups=mesh['dp'=8,'expert_0'=4,'expert_1'=4,'expert_2'=2] {'dp'}, dimensions={1}, use_global_device_ids=true | all-gather | bytes 4608 | tf_op jit(solution)/shard_map/all_gather | solution.py:50
  172.0 0.0 all-to-all-done
  172.1 155.2 %conditional.2 = (bf16[256,2048]{1,0:T(8,128)(2,1)S(1)}) conditional(s32[]{:T(128)} %convert_element_type.51, (s32[32]{0:T(128)S(1)}, s32[32,8]{1,0:T(8,128)S(1)}, s32[32,1]{1,0:T(8,128)S(1)}, s32[32,8]{1,0:T(8,128)S(1)}, f32[1024]{0:T(1024)S(1)}, /*index=5*/s32[]{:T(128)}, s32[8]{0:T(128)S(1)}, pred[32]{0:T(512)(128)(4,1)S(1)}, ...), branch_computations={%region_9.12_spmd, %region_12.15_spmd} | conditional | flops 17727356928 | bytes 85999704
  172.1 0.0 all-gather.6.cloned.1.call-start
  172.1 0.1 copy.27
  172.2 0.1 add_select_fusion.1
  172.3 0.1 eq.45
  172.4 1.3 convolution_convert_fusion.3
  173.7 0.0 all-gather.6.cloned.1.call-update
  173.7 0.2 reduce-scatter.5.cloned.1.call-start
  174.0 70.5 %all-gather.6.cloned.1.call-done = bf16[1280,2048]{1,0:T(8,128)(2,1)} async-done(((bf16[160,2048]{1,0:T(8,128)(2,1)}), bf16[1280,2048]{1,0:T(8,128)(2,1)}) %all-gather.6.cloned.1.call-update) | async-done | bytes 5242896 | tf_op jit(solution)/shard_map/cond/branch_1_fun/all_gather | solution.py:59
  244.4 16.9 %convolution_convert_fusion.2 = bf16[1280,2048]{1,0:T(8,128)(2,1)} fusion(bf16[1,1024,2048]{2,1,0:T(8,128)(2,1)} %get-tuple-element.129, bf16[1280,2048]{1,0:T(8,128)(2,1)} %all-gather.6.cloned.1.call-done, bf16[1,2048,1024]{2,1,0:T(8,128)(2,1)} %get-tuple-element.128), kind=kOutput, calls=%fused_computation.19 | convolution fusion | flops 10742661120 | bytes 18874368 | tf_op jit(solution)/shard_map/cond/branch_1_fun/dot_general | solution.py:63
  261.3 0.0 reduce-scatter.5.cloned.1.call-update
  261.4 0.7 select_reduce_fusion.1
  264.0 0.1 pad_dynamic-slice_fusion.1
  264.1 61.4 %reduce-scatter.5.cloned.1.call-done = bf16[160,2048]{1,0:T(8,128)(2,1)} async-done(((bf16[1280,2048]{1,0:T(8,128)(2,1)}), bf16[160,2048]{1,0:T(8,128)(2,1)}) %reduce-scatter.5.cloned.1.call-update) | async-done | bytes 655376 | tf_op jit(solution)/shard_map/cond/branch_1_fun/reduce_scatter | solution.py:64
  325.4 1.6 fusion.15
  327.3 24.3 %all_to_all.10 = bf16[32,8,2048]{2,1,0:T(8,128)(2,1)S(1)} all-to-all(bf16[32,8,2048]{2,1,0:T(8,128)(2,1)S(1)} %bitcast.60), channel_id=1, replica_groups=mesh['dp'=8,'expert_0'=4,'expert_1'=4,'expert_2'=2] {'expert_0','expert_..., dimensions={0} | all-to-all | bytes 2097152 | tf_op jit(solution)/shard_map/all_to_all | solution.py:79
  351.5 1.5 fusion.20
  (11 shorter events, 0.1 us)
Async XLA Ops:
  6.5 2.0 copy-start
  6.5 154.6 %copy-start.1 = (f32[1,128]{1,0:T(1,128)S(1)}, f32[1,128]{1,0:T(1,128)}, u32[]{:S(2)}) copy-start(f32[1,128]{1,0:T(1,128)} %param.13) | copy-start | bytes 1540
  10.0 162.1 %all-to-all-start = ((bf16[32,8,2048]{2,1,0:T(8,128)(2,1)}), bf16[32,8,2048]{2,1,0:T(8,128)(2,1)S(1)}, u32[]{:S(2)}, u32[]{:S(2)}) async-start(bf16[32,8,2048]{2,1,0:T(8,128)(2,1)} %fusion.21), calls=%async_computation.2 | async-start | bytes 2097152 | tf_op jit(solution)/shard_map/all_to_all | solution.py:32
  172.1 72.3 %all-gather.6.cloned.1.call-start = ((), (), s32[]{:S(2)}) async-start(), calls=%async_computation.6 | async-start | bytes 5898240 | tf_op jit(solution)/shard_map/cond/branch_1_fun/all_gather | solution.py:59
  173.7 151.7 %reduce-scatter.5.cloned.1.call-start = ((), (), s32[]{:S(2)}) async-start(), calls=%async_computation.7 | async-start | bytes 5898240 | tf_op jit(solution)/shard_map/cond/branch_1_fun/reduce_scatter | solution.py:64
Sparse Core Ops, SparseCore 0:
  174.7 69.7 all-gather.5
  261.5 63.9 reduce-scatter.4
where the time goes:
time: 360 us
  blocking collectives  176 us (49%)
  waiting for transfers between devices  132 us (37%)
  matrix products  22.7 us (6%)
  between operations  14.1 us (4%)
  starting transfers between devices  8.84 us (2%)
    psum x1, blocking collectives, on_device(): lax.psum(jnp.where(device_ids == own_expert, counts[None, :], 0), EXPERT)  127 us
    all_gather x1, waiting for transfers between devices, experts(): slot_rows = lax.all_gather(plane, 'dp', axis=0, tiled=True)  70.5 us
    reduce_scatter x1, waiting for transfers between devices, experts(): lax.psum_scatter(share.astype(jnp.bfloat16), 'dp', scatter_dimension=0, t...  61.4 us
    all_to_all x1, blocking collectives, on_device(): lax.all_to_all(sent_back.reshape(expert_count, MOST, width), EXPERT, spli...  24.3 us
    dot_general x1, matrix products, experts(): share = jnp.dot(hidden, weight_out[0], preferred_element_type=jnp.float32)  16.9 us
    psum x1, blocking collectives, on_device(): lax.psum(jnp.where(plane_ids == own_dp, jnp.sum(table, axis=0)[None, :],...  13.5 us
    all_gather x1, blocking collectives, on_device(): gates_all = lax.all_gather(gate_weights[0], 'dp', axis=0, tiled=True)  10.9 us
    all_to_all x1, starting transfers between devices, on_device(): lax.all_to_all(packed.reshape(expert_count, MOST, width), EXPERT, split_a...  8.58 us
  transfers between devices with their start and end apart: 3, of which 2 were waited for; matrix products, arithmetic and copies ran while one was open for 1% of the time, Pallas kernels for 0%

commit v1 on v0

--- a/solution.py
+++ b/solution.py
@@ -56,7 +56,9 @@
         plane = lax.dot_general(
             place_table, rows, (((0,), (0,)), ((), ())), preferred_element_type=jnp.float32
         ).astype(jnp.bfloat16)
-        slot_rows = lax.all_gather(plane, "dp", axis=0, tiled=True)
+        slot_rows = jnp.concatenate(
+            lax.all_to_all(jnp.stack([plane] * lax.axis_size("dp")), "dp", 0, 0), axis=0
+        )
         hidden = jnp.maximum(
             jnp.dot(slot_rows, weight_in[0], preferred_element_type=jnp.float32), 0.0
         ).astype(jnp.bfloat16)

time: 360 us -> 409 us (1.14)
  blocking collectives: 176 us -> 286 us
  waiting for transfers between devices: 132 us -> 71 us
    all_to_all x0 -> x1, blocking collectives: none -> 110 us  [experts(): lax.all_to_all(jnp.stack([plane] * lax.axis_size('dp')), 'dp', 0, 0)]
    all_gather x1 -> x0, waiting for transfers between devices: 70.5 us -> none  [experts(): slot_rows = lax.all_gather(plane, 'dp', axis=0, tiled=True)]
    reduce_scatter x1, waiting for transfers between devices: 61.4 us -> 71 us  [experts(): lax.psum_scatter(share.astype(jnp.bfloat16), 'dp', scatter_dimension=0, t...]
  transfers between devices with their start and end apart: 3 -> 2, of which waited for: 2 -> 1; matrix products, arithmetic and copies ran while one was open for 1% -> 0% of each run, Pallas kernels for 0% -> 0%
where the time goes in v1:
time: 409 us
  blocking collectives  286 us (70%)
  waiting for transfers between devices  71 us (17%)
  matrix products  21.9 us (5%)
  between operations  14.1 us (3%)
  starting transfers between devices  8.62 us (2%)
    psum x1, blocking collectives, on_device(): lax.psum(jnp.where(device_ids == own_expert, counts[None, :], 0), EXPERT)  127 us
    all_to_all x1, blocking collectives, experts(): lax.all_to_all(jnp.stack([plane] * lax.axis_size('dp')), 'dp', 0, 0)  110 us
    reduce_scatter x1, waiting for transfers between devices, experts(): lax.psum_scatter(share.astype(jnp.bfloat16), 'dp', scatter_dimension=0, t...  71 us
    all_to_all x1, blocking collectives, on_device(): lax.all_to_all(sent_back.reshape(expert_count, MOST, width), EXPERT, spli...  24.3 us
    dot_general x1, matrix products, experts(): share = jnp.dot(hidden, weight_out[0], preferred_element_type=jnp.float32)  16.9 us
    psum x1, blocking collectives, on_device(): lax.psum(jnp.where(plane_ids == own_dp, jnp.sum(table, axis=0)[None, :],...  13.5 us
    all_gather x1, blocking collectives, on_device(): gates_all = lax.all_gather(gate_weights[0], 'dp', axis=0, tiled=True)  10.9 us
    all_to_all x1, starting transfers between devices, on_device(): lax.all_to_all(packed.reshape(expert_count, MOST, width), EXPERT, split_a...  8.58 us
  transfers between devices with their start and end apart: 2, of which 1 were waited for; matrix products, arithmetic and copies ran while one was open for 0% of the time, Pallas kernels for 0%

profile of v1, /device:TPU:1, one launch (start us, length us, event | category | flops | bytes accessed | tf_op | source)
XLA Modules:
  0.0 408.7 jit_solution(16161367549824904006)
XLA Ops:
  6.5 0.0 copy-start
  6.5 0.0 copy-start.1
  6.5 0.9 convert_bitcast_fusion.1
  7.5 0.6 reduce-window.11
  8.1 0.2 slice_reduce_fusion
  8.3 0.1 iota.68
  8.4 0.1 convert_subtract_fusion
  8.5 0.0 copy-done
  8.5 1.5 fusion.21
  10.0 8.6 %all-to-all-start.2 = ((bf16[32,8,2048]{2,1,0:T(8,128)(2,1)}), bf16[32,8,2048]{2,1,0:T(8,128)(2,1)S(1)}, u32[]{:S(2)}, u32[]{:S(2)}) async-start(bf16[32,8,2048]{2,1,0:T(8,128)(2,1)} %fusion.21), calls=%async_computation.4 | async-start | bytes 2097152 | tf_op jit(solution)/shard_map/all_to_all | solution.py:32
  18.6 0.1 broadcast_select_fusion
  18.7 127.2 %psum.14 = s32[32,32]{1,0:T(8,128)S(1)} all-reduce(s32[32,32]{1,0:T(8,128)S(1)} %broadcast_select_fusion), channel_id=1, replica_groups=mesh['dp'=8,'expert_0'=4,'expert_1'=4,'expert_2'=2] {'expert_0','expert_..., use_global_device_ids=true, to_apply=%region_3.4 | all-reduce | flops 1024 | bytes 8192 | tf_op jit(solution)/shard_map/psum | solution.py:37
  145.9 0.1 select_reduce_fusion.2
  146.0 0.1 broadcast_select_fusion.1
  146.1 13.5 %psum.15 = s32[8,32]{1,0:T(8,128)S(1)} all-reduce(s32[8,32]{1,0:T(8,128)S(1)} %broadcast_select_fusion.1), channel_id=1, replica_groups=mesh['dp'=8,'expert_0'=4,'expert_1'=4,'expert_2'=2] {'dp'}, use_global_device_ids=true, to_apply=%region_5.6 | all-reduce | flops 256 | bytes 2048 | tf_op jit(solution)/shard_map/psum | solution.py:39
  159.6 0.7 reduce_max.9
  161.0 0.1 copy.25
  161.1 0.1 reduce-window.18
  161.2 0.0 copy-done.1
  161.2 10.9 %all-gather = f32[1,1024]{1,0:T(1,128)S(1)} all-gather(f32[1,128]{1,0:T(1,128)S(1)} %copy-done.1), channel_id=2, replica_groups=mesh['dp'=8,'expert_0'=4,'expert_1'=4,'expert_2'=2] {'dp'}, dimensions={1}, use_global_device_ids=true | all-gather | bytes 4608 | tf_op jit(solution)/shard_map/all_gather | solution.py:50
  172.0 0.0 all-to-all-done.2
  172.1 204.0 %conditional.2 = (bf16[256,2048]{1,0:T(8,128)(2,1)S(1)}) conditional(s32[]{:T(128)} %convert_element_type.51, (s32[32]{0:T(128)S(1)}, s32[32,8]{1,0:T(8,128)S(1)}, s32[32,1]{1,0:T(8,128)S(1)}, s32[32,8]{1,0:T(8,128)S(1)}, f32[1024]{0:T(1024)S(1)}, /*index=5*/s32[]{:T(128)}, s32[8]{0:T(128)S(1)}, pred[32]{0:T(512)(128)(4,1)S(1)}, ...), branch_computations={%region_9.12_spmd, %region_12.15_spmd} | conditional | flops 17727356928 | bytes 83902504
  172.1 0.0 reduce-scatter.5.cloned.1.call-start
  172.1 0.1 copy.27
  172.2 0.1 add_select_fusion.1
  172.3 0.1 eq.45
  172.4 0.5 convolution_convert_fusion.3
  172.9 0.7 stack.2
  173.5 110.1 %all_to_all.19 = bf16[8,160,2048]{2,1,0:T(8,128)(2,1)} all-to-all(bf16[8,160,2048]{2,1,0:T(8,128)(2,1)S(1)} %stack.2), channel_id=1, replica_groups=mesh['dp'=8,'expert_0'=4,'expert_1'=4,'expert_2'=2] {'dp'}, dimensions={0} | all-to-all | bytes 10485760 | tf_op jit(solution)/shard_map/cond/branch_1_fun/all_to_all | solution.py:60
  283.6 16.9 %convolution_convert_fusion.2 = bf16[1280,2048]{1,0:T(8,128)(2,1)} fusion(bf16[1,1024,2048]{2,1,0:T(8,128)(2,1)} %get-tuple-element.129, bf16[1280,2048]{1,0:T(8,128)(2,1)} %bitcast.63, bf16[1,2048,1024]{2,1,0:T(8,128)(2,1)} %get-tuple-element.128), kind=kOutput, calls=%fused_computation.19 | convolution fusion | flops 10742661120 | bytes 18874368 | tf_op jit(solution)/shard_map/cond/branch_1_fun/dot_general | solution.py:65
  300.5 0.0 reduce-scatter.5.cloned.1.call-update
  300.5 0.7 select_reduce_fusion.1
  303.2 0.1 pad_dynamic-slice_fusion.1
  303.3 71.0 %reduce-scatter.5.cloned.1.call-done = bf16[160,2048]{1,0:T(8,128)(2,1)} async-done(((bf16[1280,2048]{1,0:T(8,128)(2,1)}), bf16[160,2048]{1,0:T(8,128)(2,1)}) %reduce-scatter.5.cloned.1.call-update) | async-done | bytes 655376 | tf_op jit(solution)/shard_map/cond/branch_1_fun/reduce_scatter | solution.py:66
  374.2 1.6 fusion.15
  376.1 24.3 %all_to_all.20 = bf16[32,8,2048]{2,1,0:T(8,128)(2,1)S(1)} all-to-all(bf16[32,8,2048]{2,1,0:T(8,128)(2,1)S(1)} %bitcast.64), channel_id=1, replica_groups=mesh['dp'=8,'expert_0'=4,'expert_1'=4,'expert_2'=2] {'expert_0','expert_..., dimensions={0} | all-to-all | bytes 2097152 | tf_op jit(solution)/shard_map/all_to_all | solution.py:81
  400.3 1.5 fusion.20
  (11 shorter events, 0.1 us)
Async XLA Ops:
  6.5 2.0 copy-start
  6.5 154.6 %copy-start.1 = (f32[1,128]{1,0:T(1,128)S(1)}, f32[1,128]{1,0:T(1,128)}, u32[]{:S(2)}) copy-start(f32[1,128]{1,0:T(1,128)} %param.13) | copy-start | bytes 1540
  10.0 162.1 %all-to-all-start.2 = ((bf16[32,8,2048]{2,1,0:T(8,128)(2,1)}), bf16[32,8,2048]{2,1,0:T(8,128)(2,1)S(1)}, u32[]{:S(2)}, u32[]{:S(2)}) async-start(bf16[32,8,2048]{2,1,0:T(8,128)(2,1)} %fusion.21), calls=%async_computation.4 | async-start | bytes 2097152 | tf_op jit(solution)/shard_map/all_to_all | solution.py:32
  172.1 202.2 %reduce-scatter.5.cloned.1.call-start = ((), (), s32[]{:S(2)}) async-start(), calls=%async_computation.7 | async-start | bytes 5898240 | tf_op jit(solution)/shard_map/cond/branch_1_fun/reduce_scatter | solution.py:66
Sparse Core Ops, SparseCore 0:
  300.6 73.5 reduce-scatter.4
